TPU v7x, 256 devices: a whole 4x4x8 slice. The times are simulated.
256 devices in a mesh: ulysses: 16 (over z, x_hi), blk: 16 (over y, x_lo, core).
Axes of the slice: x: 4 (x_hi: 2, x_lo: 2; x = x_hi * 2 + x_lo), y: 4, z: 8, core: 2. Of those that a mesh axis runs over, the one named last changes fastest.
Arguments:
- queries: bfloat16 [16, 1024, 4096], P('blk', 'ulysses'), may hold values from -6 to 6
- key_rows: bfloat16 [16, 1024, 1024], P('blk', 'ulysses'), may hold values from -6 to 6
- value_rows: bfloat16 [16, 1024, 1024], P('blk', 'ulysses'), may hold values from -6 to 6
- tile_segment: int32 [128], replicated, may hold values from 0 to 31, never falling along the last dimension, each value on 1 to 8 neighbouring positions
Outputs:
- attended: bfloat16 [16, 1024, 4096], P('blk', 'ulysses')
Inputs may be any that keep to these rules, and one draw needn't show every extreme that they name: `tile_segment`: segment numbers never fall along the sequence and each segment covers 1 to 8 tiles.
All inputs are finite; a program needn't handle non-finite values.
Results may differ from a plain program's by a relative error of at most 0.0045.
Values may be sent and summed in bfloat16 or wider, within the bound.
No kernel may reach another device: no remote copies, remote signals or barrier semaphores. Data moves between devices by JAX's collectives and lax.ppermute only.
A program may use at most 64 MiB of HBM per device.

v0:
```python
import math

import jax
import jax.numpy as jnp
from jax import lax
from jax.experimental import pallas as pl
from jax.experimental.pallas import tpu as pltpu
from jax.sharding import Mesh, PartitionSpec as P


HEAD_DIM = 128
TILE = 128
HALF = 512
COLS = 1024
MASKED = -1e30
SLACK = 60.0
OFFS = (0, -1, 1, 2)
PLANE = ("xh", "y", "xl", "core")
ROUND = ("z", "y", "xl", "core")
TEAMS = [[z * 16 + (n if z < 4 else 15 - n) for z in range(8)] for n in range(16)]


def exchange(rows):
    return lax.all_to_all(
        rows, ROUND, split_axis=0, concat_axis=0, axis_index_groups=TEAMS, tiled=True
    )


def plane_perm(step, x_core):
    pairs = []
    for xh in range(2):
        for y in range(4):
            for xl in range(2):
                for core in range(2):
                    x = xh * 2 + xl
                    tx, ty = ((x + step) % 4, y) if core == x_core else (x, (y + step) % 4)
                    src = ((xh * 4 + y) * 2 + xl) * 2 + core
                    dst = (((tx // 2) * 4 + ty) * 2 + tx % 2) * 2 + core
                    pairs.append((src, dst))
    return pairs


def ring_near(rows, x_core):
    return (
        lax.ppermute(rows, PLANE, plane_perm(1, x_core)),
        lax.ppermute(rows, PLANE, plane_perm(-1, x_core)),
    )


def ring_far(right, left, x_core):
    half = right.shape[0] // 2
    return (
        lax.ppermute(right[:half], PLANE, plane_perm(1, x_core)),
        lax.ppermute(left[half:], PLANE, plane_perm(-1, x_core)),
    )


def swap(rows):
    return lax.ppermute(rows, "core", [(0, 1), (1, 0)])


ALL8 = [(o, j) for o in range(4) for j in range(2)]
PARTS = (
    (0, 0, 0, ALL8, 0),
    (1, 0, 1, ALL8, 2), (2, 0, 2, ALL8, 4),
    (1, 1, 1, ALL8, 6), (2, 1, 2, ALL8, 6),
    (0, 1, 0, ALL8, 10), (3, 1, 3, ALL8[:4], 10), (4, 1, 3, ALL8[4:], 10),
    (3, 0, 3, ALL8[:4], 14), (4, 0, 3, ALL8[4:], 14),
)


def attend(seg_ref, idx_ref, q_ref, self_ref, *rest):
    own_refs, swp_refs = rest[:5], rest[5:10]
    o_ref, buf, qs, hbs, far, flag, sems, acc, mx, over, lim = rest[10:]
    z, xh, xl, y, core = [idx_ref[k] for k in range(5)]
    flip = jnp.where(z < 4, 0, 15)
    x = xh * 2 + xl
    n = (y * 4 + xl * 2 + core) ^ flip

    for op, half, o2, pieces, base in PARTS:
        for i, (o1, j) in enumerate(pieces):
            dx, dy = (OFFS[o1], OFFS[o2]) if half == 0 else (OFFS[o2], OFFS[o1])
            sx, sy = (x + dx) & 3, (y + dy) & 3
            cc = half ^ j
            pair = base + (sx & 1 if half == 0 else sy)
            block = (sy * 4 + (sx & 1) * 2 + cc) ^ flip ^ (15 * half)
            hbs[pair * 2 + cc] = block * 2 + half
            slot = pair * 4 + cc * 2 + (sx >> 1)

            @pl.when(core == half)
            def _():
                pltpu.make_async_copy(
                    own_refs[op].at[pl.ds(i * 256, 256)], buf.at[slot], sems.at[slot]
                ).start()

            @pl.when(core != half)
            def _():
                pltpu.make_async_copy(
                    swp_refs[op].at[pl.ds(i * 256, 256)], buf.at[slot], sems.at[slot]
                ).start()

    scale = HEAD_DIM ** -0.5 * math.log2(math.e)
    for g in range(2):
        reach = n * 2 if g == 0 else (15 - n) * 2 + 1
        for t in range(4):
            rows = q_ref[g * 4 + t].astype(jnp.float32) * scale
            cols = jnp.concatenate([rows[:, h * 128:(h + 1) * 128] for h in range(4)], axis=0).T
            keys = self_ref[g * 4 + t][:, :128].astype(jnp.float32)
            keys = jnp.concatenate([keys] * 4, axis=0).T
            hi = cols.astype(jnp.bfloat16)
            lo = (cols - hi.astype(jnp.float32)).astype(jnp.bfloat16)
            at = slice(t * 256, (t + 1) * 256)
            qs[g, :, at] = jnp.concatenate([hi, lo], axis=0)
            mx[g, :, at] = jnp.sum(cols * keys, axis=0, keepdims=True)
            qt = (n if g == 0 else 15 - n) * 8 + g * 4 + t
            seg = seg_ref[qt]
            end = qt
            for d in range(1, 8):
                nxt = jnp.minimum(qt + d, 127)
                end = end + jnp.where((seg_ref[nxt] == seg) & (qt + d < 128), 1, 0)
            limit = jnp.where((seg & 1) == 1, (end + 1) * TILE - 1, -1)
            reach = jnp.maximum(reach, limit // HALF)
            col = lax.broadcasted_iota(jnp.int32, (1, 256), 1)
            lim[g, :, at] = jnp.maximum(qt * TILE + xh * 64 + (col & 63), limit)
        far[g] = reach
    acc[...] = jnp.zeros_like(acc)

    def load(slot, count):
        rows = buf[pl.ds(slot, count)].reshape(count * 256, 256)
        keys = rows[:, :128]
        ones = jnp.ones((16, count * 256), jnp.bfloat16)
        return (
            jnp.concatenate([keys, keys], axis=1),
            jnp.concatenate([rows[:, 128:].T, ones], axis=0),
        )

    def scores(g, kk, mask):
        s = jnp.dot(kk, qs[g], preferred_element_type=jnp.float32)
        return s if mask is None else jnp.where(mask, s, MASKED)

    def by_sublane(a):
        return a.reshape(a.shape[0] // 8, 8, COLS)

    def quick(g, kk, vt, mask):
        ref = mx[g]
        s = scores(g, kk, mask)
        top = jnp.max(by_sublane(s), axis=0)
        p = jnp.exp2(s - ref)
        pv = jnp.dot(vt, p.astype(jnp.bfloat16), preferred_element_type=jnp.float32)
        top = jnp.max(top, axis=0, keepdims=True) - ref
        over[...] = top
        good = top <= SLACK
        acc[g] = acc[g] + jnp.where(good, pv, 0.0)
        flag[0] = (jnp.max(top) > SLACK).astype(jnp.int32)

    def slow(g, kk, vt, mask):
        todo = over[...] > SLACK
        s = scores(g, kk, mask)
        old = mx[g]
        new = jnp.where(todo, jnp.maximum(old, jnp.max(s, axis=0, keepdims=True)), old)
        alpha = jnp.exp2(old - new)
        p = jnp.where(todo, jnp.exp2(s - new), 0.0)
        pv = jnp.dot(vt, p.astype(jnp.bfloat16), preferred_element_type=jnp.float32)
        acc[g] = acc[g] * alpha + pv
        mx[g] = new

    def both(g, slot, count, mask):
        quick(g, *load(slot, count), mask)

        @pl.when(flag[0] == 1)
        def _():
            slow(g, *load(slot, count), mask)

    def one_pair(p, c):
        for i in range(4):
            pltpu.make_async_copy(
                own_refs[0].at[pl.ds(0, 256)], buf.at[p * 4 + i], sems.at[p * 4 + i]
            ).wait()
        hb0, hb1 = hbs[p * 2], hbs[p * 2 + 1]

        def one_group(g, c):
            hbq = jnp.where(g == 0, n * 2, (15 - n) * 2 + 1)
            dense = (hb0 < hbq) & (hb1 < hbq)

            @pl.when(dense)
            def _():
                both(g, p * 4, 4, None)

            @pl.when(jnp.logical_not(dense))
            def _():
                def masked(u, c):
                    hb = hbs[p * 2 + u]

                    @pl.when(hb <= far[g])
                    def _():
                        key = lax.broadcasted_iota(jnp.int32, (HALF, 128), 0)
                        kpos = hb * HALF + ((key & 255) >> 6) * TILE + (key >> 8) * 64 + (key & 63)
                        kpos = jnp.concatenate([kpos] * (COLS // 128), axis=1)
                        both(g, p * 4 + u * 2, 2, kpos <= lim[g])

                    return c

                lax.fori_loop(0, 2, masked, 0)

            return c

        lax.fori_loop(0, 2, one_group, 0)
        return c

    lax.fori_loop(0, 16, one_pair, 0)

    for t in range(8):
        at = slice(t % 4 * 256, (t % 4 + 1) * 256)
        total = acc[t // 4, 128:129, at]
        o = (acc[t // 4, :128, at] / total).T.astype(jnp.bfloat16)
        o_ref[t] = jnp.concatenate([o[h * 64:(h + 1) * 64] for h in range(4)], axis=1)


def local(queries, key_rows, value_rows, tile_segment):
    z, xh, xl, y, core = [lax.axis_index(a) for a in ("z", "xh", "xl", "y", "core")]
    q = queries[0].reshape(64, 8, 512)
    k = key_rows[0].reshape(64, 8, 128)
    v = value_rows[0].reshape(64, 8, 128)
    kept_kv = exchange(jnp.transpose(jnp.concatenate([k, v], axis=2), (1, 0, 2)))
    kv = kept_kv.reshape(512, 256)
    idx = jnp.stack([z, xh, xl, y, core]).astype(jnp.int32)

    kept = lax.dynamic_slice_in_dim(kv, core * 256, 256, 0)
    sent = lax.dynamic_slice_in_dim(kv, (1 - core) * 256, 256, 0)
    start = jnp.concatenate([kept, swap(sent)], axis=0)
    q = jnp.transpose(q, (1, 0, 2))
    q, start = lax.optimization_barrier((q, start))
    q = exchange(q)
    r1, l1 = ring_near(start, 0)
    f1 = ring_far(r1, l1, 0)
    row = jnp.concatenate([start, r1, l1, *f1], axis=0)
    r2, l2 = ring_near(row, 1)
    row_s = swap(row)
    f2 = ring_far(r2, l2, 1)
    own = (row, r2, l2, *f2)
    swp = (row_s, *[swap(o) for o in own[1:]])

    smem = pl.BlockSpec(memory_space=pltpu.SMEM)
    vmem = pl.BlockSpec(memory_space=pltpu.VMEM)
    out = pl.pallas_call(
        attend,
        out_shape=jax.ShapeDtypeStruct((8, 64, 512), jnp.bfloat16),
        in_specs=[smem, smem, vmem, vmem] + [pl.BlockSpec(memory_space=pl.ANY)] * 10,
        out_specs=vmem,
        scratch_shapes=[
            pltpu.VMEM((64, 256, 256), jnp.bfloat16),
            pltpu.VMEM((2, 256, COLS), jnp.bfloat16),
            pltpu.SMEM((32,), jnp.int32),
            pltpu.SMEM((2,), jnp.int32),
            pltpu.SMEM((1,), jnp.int32),
            pltpu.SemaphoreType.DMA((64,)),
            pltpu.VMEM((2, 144, COLS), jnp.float32),
            pltpu.VMEM((2, 1, COLS), jnp.float32),
            pltpu.VMEM((1, COLS), jnp.float32),
            pltpu.VMEM((2, 1, COLS), jnp.int32),
        ],
        name="attend",
    )(tile_segment, idx, q, kept_kv, *own, *swp)

    out = exchange(out)
    return jnp.transpose(out, (1, 0, 2)).reshape(1, 64, 4096)


def solution(mesh):
    fine = Mesh(mesh.devices.reshape(8, 2, 4, 2, 2), ("z", "xh", "y", "xl", "core"))
    split = P(("y", "xl", "core"), ("z", "xh"), None)

    return jax.shard_map(
        local, mesh=fine, in_specs=(split, split, split, P()), out_specs=split, check_vma=False
    )
```

profile of v0, /device:TPU:1, one launch (start us, length us, event | category | flops | bytes accessed | tf_op | source)
XLA Modules:
  0.0 142.2 jit_solution(8703625298776951422)
XLA Ops:
  0.0 0.9 copy.10
  1.0 0.9 copy-done.6
  2.6 13.1 %all-to-all-start = ((bf16[8,64,256]{2,1,0:T(8,128)(2,1)}), bf16[8,64,256]{2,1,0:T(8,128)(2,1)S(1)}, u32[]{:S(2)}, u32[]{:S(2)}) async-start(bf16[8,64,256]{2,1,0:T(8,128)(2,1)} %maximum_bitcast_fusion), calls=%async_computation | async-start | bytes 524288 | tf_op jit(solution)/shard_map/all_to_all | solution.py:24
  15.7 13.2 %all-to-all-done.self_ref = bf16[8,64,256]{2,1,0:T(8,128)(2,1)S(1)} async-done(((bf16[8,64,256]{2,1,0:T(8,128)(2,1)}), bf16[8,64,256]{2,1,0:T(8,128)(2,1)S(1)}, u32[]{:S(2)}, u32[]{:S(2)}) %all-to-all-start) | async-done | bytes 262176 | tf_op jit(solution)/shard_map/all_to_all | solution.py:24
  29.8 0.9 copy.13
  31.0 1.8 %collective-permute-start.2 = (bf16[512,256]{1,0:T(8,128)(2,1)S(1)}, bf16[512,256]{1,0:T(8,128)(2,1)S(1)}, u32[]{:S(2)}, u32[]{:S(2)}) collective-permute-start(bf16[512,256]{1,0:T(8,128)(2,1)S(1)} %pad_maximum_fusion), channel_id=1, source_target_pairs={{0,18},{1,13},{2,0},{3,15},{4,22},{5,1},{6,4},{7,3},{8,26},{9,5},{... | collective-permute-start | bytes 786440 | tf_op jit(solution)/shard_map/ppermute | solution.py:46
  33.5 3.1 %collective-permute-done.2 = bf16[512,256]{1,0:T(8,128)(2,1)S(1)} collective-permute-done((bf16[512,256]{1,0:T(8,128)(2,1)S(1)}, bf16[512,256]{1,0:T(8,128)(2,1)S(1)}, u32[]{:S(2)}, u32[]{:S(2)}) %collective-permute-start.2) | collective-permute-done | bytes 262176 | tf_op jit(solution)/shard_map/ppermute | solution.py:46
  36.6 3.0 %collective-permute-start.4 = (bf16[256,256]{1,0:T(8,128)(2,1)S(1)}, bf16[256,256]{1,0:T(8,128)(2,1)S(1)}, u32[]{:S(2)}, u32[]{:S(2)}) collective-permute-start(bf16[256,256]{1,0:T(8,128)(2,1)S(1)} %slice.17), channel_id=1, source_target_pairs={{0,18},{1,13},{2,0},{3,15},{4,22},{5,1},{6,4},{7,3},{8,26},{9,5},{... | collective-permute-start | bytes 393224 | tf_op jit(solution)/shard_map/ppermute | solution.py:54
  41.1 3.6 %collective-permute-done.3 = bf16[256,256]{1,0:T(8,128)(2,1)S(1)} collective-permute-done((bf16[256,256]{1,0:T(8,128)(2,1)S(1)}, bf16[256,256]{1,0:T(8,128)(2,1)S(1)}, u32[]{:S(2)}, u32[]{:S(2)}) %collective-permute-start.3) | collective-permute-done | bytes 131104 | tf_op jit(solution)/shard_map/ppermute | solution.py:53
  46.0 1.3 collective-permute-start.6
  47.5 3.8 %collective-permute-start.9 = (bf16[2048,256]{1,0:T(8,128)(2,1)}, bf16[2048,256]{1,0:T(8,128)(2,1)}, u32[]{:S(2)}, u32[]{:S(2)}) collective-permute-start(bf16[2048,256]{1,0:T(8,128)(2,1)} %constant_dynamic-update-slice_fusion.rest_0_), channel_id=1, source_target_pairs={{0,1},{1,0},{2,3},{3,2},{4,5},{5,4},{6,7},{7,6},{8,9},{9,8},{10,11... | collective-permute-start | bytes 3145736 | tf_op jit(solution)/shard_map/ppermute | solution.py:59
  51.3 8.9 %collective-permute-done.6.rest_2_ = bf16[2048,256]{1,0:T(8,128)(2,1)S(1)} collective-permute-done((bf16[2048,256]{1,0:T(8,128)(2,1)}, bf16[2048,256]{1,0:T(8,128)(2,1)S(1)}, u32[]{:S(2)}, u32[]{:S(2)}) %collective-permute-start.6) | collective-permute-done | bytes 1048608 | tf_op jit(solution)/shard_map/ppermute | solution.py:46
  60.2 0.9 slice.19
  61.1 2.5 %collective-permute-start.8 = (bf16[1024,256]{1,0:T(8,128)(2,1)}, bf16[1024,256]{1,0:T(8,128)(2,1)S(1)}, u32[]{:S(2)}, u32[]{:S(2)}) collective-permute-start(bf16[1024,256]{1,0:T(8,128)(2,1)} %slice.19), channel_id=1, source_target_pairs={{0,12},{1,19},{2,14},{3,1},{4,0},{5,23},{6,2},{7,5},{8,4},{9,27},{... | collective-permute-start | bytes 1572872 | tf_op jit(solution)/shard_map/ppermute | solution.py:54
  63.6 3.4 %collective-permute-start.11 = (bf16[2048,256]{1,0:T(8,128)(2,1)S(1)}, bf16[2048,256]{1,0:T(8,128)(2,1)}, u32[]{:S(2)}, u32[]{:S(2)}) collective-permute-start(bf16[2048,256]{1,0:T(8,128)(2,1)S(1)} %collective-permute-done.6.rest_2_), channel_id=1, source_target_pairs={{0,1},{1,0},{2,3},{3,2},{4,5},{5,4},{6,7},{7,6},{8,9},{9,8},{10,11... | collective-permute-start | bytes 3145736 | tf_op jit(solution)/shard_map/ppermute | solution.py:59
  67.0 1.0 slice.18
  68.3 3.8 %all-to-all-start.1 = ((bf16[8,64,512]{2,1,0:T(8,128)(2,1)}), bf16[8,64,512]{2,1,0:T(8,128)(2,1)S(1)}, u32[]{:S(2)}, u32[]{:S(2)}) async-start(bf16[8,64,512]{2,1,0:T(8,128)(2,1)} %bitcast.20), calls=%async_computation.1 | async-start | bytes 1048576 | tf_op jit(solution)/shard_map/all_to_all | solution.py:24
  72.1 2.5 %collective-permute-start.13 = (bf16[1024,256]{1,0:T(8,128)(2,1)S(1)}, bf16[1024,256]{1,0:T(8,128)(2,1)}, u32[]{:S(2)}, u32[]{:S(2)}) collective-permute-start(bf16[1024,256]{1,0:T(8,128)(2,1)S(1)} %collective-permute-done.8.rest_4_), channel_id=1, source_target_pairs={{0,1},{1,0},{2,3},{3,2},{4,5},{5,4},{6,7},{7,6},{8,9},{9,8},{10,11... | collective-permute-start | bytes 1572872 | tf_op jit(solution)/shard_map/ppermute | solution.py:59
  74.6 3.3 %collective-permute-done.7.rest_3_ = bf16[1024,256]{1,0:T(8,128)(2,1)} collective-permute-done((bf16[1024,256]{1,0:T(8,128)(2,1)}, bf16[1024,256]{1,0:T(8,128)(2,1)}, u32[]{:S(2)}, u32[]{:S(2)}) %collective-permute-start.7) | collective-permute-done | bytes 524320 | tf_op jit(solution)/shard_map/ppermute | solution.py:53
  77.9 1.4 collective-permute-start.12
  79.8 12.4 %all-to-all-done.1.q_ref = bf16[8,64,512]{2,1,0:T(8,128)(2,1)S(1)} async-done(((bf16[8,64,512]{2,1,0:T(8,128)(2,1)}), bf16[8,64,512]{2,1,0:T(8,128)(2,1)S(1)}, u32[]{:S(2)}, u32[]{:S(2)}) %all-to-all-start.1) | async-done | bytes 524320 | tf_op jit(solution)/shard_map/all_to_all | solution.py:24
  93.0 25.7 %attend.1 = bf16[8,64,512]{2,1,0:T(8,128)(2,1)} custom-call(s32[128]{0:T(128)} %seg_ref.1, s32[5]{0:T(128)} %stack.23.idx_ref, bf16[8,64,512]{2,1,0:T(8,128)(2,1)} %copy-done.3, bf16[8,64,256]{2,1,0:T(8,128)(2,1)} %copy-done.2, bf16[2048,256]{1,0:T(8,128)(2,1)} %constant_dynamic-update-slice_fusion.rest_0_, bf16[2048,256]{1,0:T(8,128)(2,1)} %copy-done.1, ...), custom_call_target="tpu_custom_call" | custom-call | tf_op jit(solution)/shard_map/attend/pallas_call | solution.py:245
  118.7 22.1 %all_to_all.15 = bf16[8,64,512]{2,1,0:T(8,128)(2,1)S(1)} all-to-all(bf16[8,64,512]{2,1,0:T(8,128)(2,1)} %attend.1), channel_id=1, replica_groups={{0,32,64,96,143,175,207,239},{1,33,65,97,142,174,206,238},{2,34,66,98,1..., dimensions={0} | all-to-all | bytes 1048576 | tf_op jit(solution)/shard_map/all_to_all | solution.py:24
  141.1 1.0 reshape.7
  (45 shorter events, 7.6 us)
Async XLA Ops:
  0.9 0.9 copy-start.6
  2.6 27.0 %copy-start.5 = (bf16[1,64,4096]{2,1,0:T(8,128)(2,1)S(1)}, bf16[1,64,4096]{2,1,0:T(8,128)(2,1)}, u32[]{:S(2)}) copy-start(bf16[1,64,4096]{2,1,0:T(8,128)(2,1)} %param.4) | copy-start | bytes 1572868
  2.6 26.3 %all-to-all-start = ((bf16[8,64,256]{2,1,0:T(8,128)(2,1)}), bf16[8,64,256]{2,1,0:T(8,128)(2,1)S(1)}, u32[]{:S(2)}, u32[]{:S(2)}) async-start(bf16[8,64,256]{2,1,0:T(8,128)(2,1)} %maximum_bitcast_fusion), calls=%async_computation | async-start | bytes 524288 | tf_op jit(solution)/shard_map/all_to_all | solution.py:24
  28.9 0.7 copy-start.2
  29.6 1.3 collective-permute-start
  31.0 5.6 %collective-permute-start.2 = (bf16[512,256]{1,0:T(8,128)(2,1)S(1)}, bf16[512,256]{1,0:T(8,128)(2,1)S(1)}, u32[]{:S(2)}, u32[]{:S(2)}) collective-permute-start(bf16[512,256]{1,0:T(8,128)(2,1)S(1)} %pad_maximum_fusion), channel_id=1, source_target_pairs={{0,18},{1,13},{2,0},{3,15},{4,22},{5,1},{6,4},{7,3},{8,26},{9,5},{... | collective-permute-start | bytes 786440 | tf_op jit(solution)/shard_map/ppermute | solution.py:46
  32.7 6.8 %collective-permute-start.1 = (bf16[512,256]{1,0:T(8,128)(2,1)S(1)}, bf16[512,256]{1,0:T(8,128)(2,1)S(1)}, u32[]{:S(2)}, u32[]{:S(2)}) collective-permute-start(bf16[512,256]{1,0:T(8,128)(2,1)S(1)} %pad_maximum_fusion), channel_id=1, source_target_pairs={{0,2},{1,5},{2,16},{3,7},{4,6},{5,9},{6,20},{7,11},{8,10},{9,13},{... | collective-permute-start | bytes 786440 | tf_op jit(solution)/shard_map/ppermute | solution.py:45
  36.6 8.8 %collective-permute-start.4 = (bf16[256,256]{1,0:T(8,128)(2,1)S(1)}, bf16[256,256]{1,0:T(8,128)(2,1)S(1)}, u32[]{:S(2)}, u32[]{:S(2)}) collective-permute-start(bf16[256,256]{1,0:T(8,128)(2,1)S(1)} %slice.17), channel_id=1, source_target_pairs={{0,18},{1,13},{2,0},{3,15},{4,22},{5,1},{6,4},{7,3},{8,26},{9,5},{... | collective-permute-start | bytes 393224 | tf_op jit(solution)/shard_map/ppermute | solution.py:54
  39.6 5.1 %collective-permute-start.3 = (bf16[256,256]{1,0:T(8,128)(2,1)S(1)}, bf16[256,256]{1,0:T(8,128)(2,1)S(1)}, u32[]{:S(2)}, u32[]{:S(2)}) collective-permute-start(bf16[256,256]{1,0:T(8,128)(2,1)S(1)} %slice.16), channel_id=1, source_target_pairs={{0,2},{1,5},{2,16},{3,7},{4,6},{5,9},{6,20},{7,11},{8,10},{9,13},{... | collective-permute-start | bytes 393224 | tf_op jit(solution)/shard_map/ppermute | solution.py:53
  46.0 14.2 %collective-permute-start.6 = (bf16[2048,256]{1,0:T(8,128)(2,1)}, bf16[2048,256]{1,0:T(8,128)(2,1)S(1)}, u32[]{:S(2)}, u32[]{:S(2)}) collective-permute-start(bf16[2048,256]{1,0:T(8,128)(2,1)} %constant_dynamic-update-slice_fusion.rest_0_), channel_id=1, source_target_pairs={{0,12},{1,19},{2,14},{3,1},{4,0},{5,23},{6,2},{7,5},{8,4},{9,27},{... | collective-permute-start | bytes 3145736 | tf_op jit(solution)/shard_map/ppermute | solution.py:46
  47.3 19.7 %collective-permute-start.5 = (bf16[2048,256]{1,0:T(8,128)(2,1)}, bf16[2048,256]{1,0:T(8,128)(2,1)S(1)}, u32[]{:S(2)}, u32[]{:S(2)}) collective-permute-start(bf16[2048,256]{1,0:T(8,128)(2,1)} %constant_dynamic-update-slice_fusion.rest_0_), channel_id=1, source_target_pairs={{0,4},{1,3},{2,6},{3,17},{4,8},{5,7},{6,10},{7,21},{8,12},{9,11},{... | collective-permute-start | bytes 3145736 | tf_op jit(solution)/shard_map/ppermute | solution.py:45
  47.5 44.8 %collective-permute-start.9 = (bf16[2048,256]{1,0:T(8,128)(2,1)}, bf16[2048,256]{1,0:T(8,128)(2,1)}, u32[]{:S(2)}, u32[]{:S(2)}) collective-permute-start(bf16[2048,256]{1,0:T(8,128)(2,1)} %constant_dynamic-update-slice_fusion.rest_0_), channel_id=1, source_target_pairs={{0,1},{1,0},{2,3},{3,2},{4,5},{5,4},{6,7},{7,6},{8,9},{9,8},{10,11... | collective-permute-start | bytes 3145736 | tf_op jit(solution)/shard_map/ppermute | solution.py:59
  60.2 7.8 %copy-start = (bf16[2048,256]{1,0:T(8,128)(2,1)}, bf16[2048,256]{1,0:T(8,128)(2,1)S(1)}, u32[]{:S(2)}) copy-start(bf16[2048,256]{1,0:T(8,128)(2,1)S(1)} %collective-permute-done.6.rest_2_) | copy-start | bytes 3145732
  61.1 11.0 %collective-permute-start.8 = (bf16[1024,256]{1,0:T(8,128)(2,1)}, bf16[1024,256]{1,0:T(8,128)(2,1)S(1)}, u32[]{:S(2)}, u32[]{:S(2)}) collective-permute-start(bf16[1024,256]{1,0:T(8,128)(2,1)} %slice.19), channel_id=1, source_target_pairs={{0,12},{1,19},{2,14},{3,1},{4,0},{5,23},{6,2},{7,5},{8,4},{9,27},{... | collective-permute-start | bytes 1572872 | tf_op jit(solution)/shard_map/ppermute | solution.py:54
  63.6 28.6 %collective-permute-start.11 = (bf16[2048,256]{1,0:T(8,128)(2,1)S(1)}, bf16[2048,256]{1,0:T(8,128)(2,1)}, u32[]{:S(2)}, u32[]{:S(2)}) collective-permute-start(bf16[2048,256]{1,0:T(8,128)(2,1)S(1)} %collective-permute-done.6.rest_2_), channel_id=1, source_target_pairs={{0,1},{1,0},{2,3},{3,2},{4,5},{5,4},{6,7},{7,6},{8,9},{9,8},{10,11... | collective-permute-start | bytes 3145736 | tf_op jit(solution)/shard_map/ppermute | solution.py:59
  67.0 1.2 copy-start.1
  68.0 24.2 %collective-permute-start.10 = (bf16[2048,256]{1,0:T(8,128)(2,1)S(1)}, bf16[2048,256]{1,0:T(8,128)(2,1)}, u32[]{:S(2)}, u32[]{:S(2)}) collective-permute-start(bf16[2048,256]{1,0:T(8,128)(2,1)S(1)} %collective-permute-done.5.rest_1_), channel_id=1, source_target_pairs={{0,1},{1,0},{2,3},{3,2},{4,5},{5,4},{6,7},{7,6},{8,9},{9,8},{10,11... | collective-permute-start | bytes 3145736 | tf_op jit(solution)/shard_map/ppermute | solution.py:59
  68.0 9.9 %collective-permute-start.7 = (bf16[1024,256]{1,0:T(8,128)(2,1)}, bf16[1024,256]{1,0:T(8,128)(2,1)}, u32[]{:S(2)}, u32[]{:S(2)}) collective-permute-start(bf16[1024,256]{1,0:T(8,128)(2,1)} %slice.18), channel_id=1, source_target_pairs={{0,4},{1,3},{2,6},{3,17},{4,8},{5,7},{6,10},{7,21},{8,12},{9,11},{... | collective-permute-start | bytes 1572872 | tf_op jit(solution)/shard_map/ppermute | solution.py:53
  68.3 24.0 %all-to-all-start.1 = ((bf16[8,64,512]{2,1,0:T(8,128)(2,1)}), bf16[8,64,512]{2,1,0:T(8,128)(2,1)S(1)}, u32[]{:S(2)}, u32[]{:S(2)}) async-start(bf16[8,64,512]{2,1,0:T(8,128)(2,1)} %bitcast.20), calls=%async_computation.1 | async-start | bytes 1048576 | tf_op jit(solution)/shard_map/all_to_all | solution.py:24
  72.1 20.2 %copy-start.4 = (bf16[1024,256]{1,0:T(8,128)(2,1)}, bf16[1024,256]{1,0:T(8,128)(2,1)S(1)}, u32[]{:S(2)}) copy-start(bf16[1024,256]{1,0:T(8,128)(2,1)S(1)} %collective-permute-done.8.rest_4_) | copy-start | bytes 1572868
  72.1 20.2 %collective-permute-start.13 = (bf16[1024,256]{1,0:T(8,128)(2,1)S(1)}, bf16[1024,256]{1,0:T(8,128)(2,1)}, u32[]{:S(2)}, u32[]{:S(2)}) collective-permute-start(bf16[1024,256]{1,0:T(8,128)(2,1)S(1)} %collective-permute-done.8.rest_4_), channel_id=1, source_target_pairs={{0,1},{1,0},{2,3},{3,2},{4,5},{5,4},{6,7},{7,6},{8,9},{9,8},{10,11... | collective-permute-start | bytes 1572872 | tf_op jit(solution)/shard_map/ppermute | solution.py:59
  77.9 14.4 %collective-permute-start.12 = (bf16[1024,256]{1,0:T(8,128)(2,1)}, bf16[1024,256]{1,0:T(8,128)(2,1)}, u32[]{:S(2)}, u32[]{:S(2)}) collective-permute-start(bf16[1024,256]{1,0:T(8,128)(2,1)} %collective-permute-done.7.rest_3_), channel_id=1, source_target_pairs={{0,1},{1,0},{2,3},{3,2},{4,5},{5,4},{6,7},{7,6},{8,9},{9,8},{10,11... | collective-permute-start | bytes 1572872 | tf_op jit(solution)/shard_map/ppermute | solution.py:59
  92.2 0.8 copy-start.3
where the time goes:
time: 143 us; the launch traced here: 142 us
  waiting for transfers between devices  44.7 us (31%)
  starting transfers between devices  36.8 us (26%)
  Pallas kernels  25.7 us (18%)
  blocking collectives  22.1 us (15%)
  local copies, waits for them, and re-layouts  12 us (8%)
    pallas_call x1, Pallas kernels, local(): pl.pallas_call(attend, out_shape=jax.ShapeDtypeStruct((8, 64, 512), jnp.b...  25.7 us
    all_to_all x2, waiting for transfers between devices, exchange(): lax.all_to_all(rows, ROUND, split_axis=0, concat_axis=0, axis_index_group...  25.6 us
    all_to_all x1, blocking collectives, exchange(): lax.all_to_all(rows, ROUND, split_axis=0, concat_axis=0, axis_index_group...  22.1 us
    all_to_all x2, starting transfers between devices, exchange(): lax.all_to_all(rows, ROUND, split_axis=0, concat_axis=0, axis_index_group...  16.9 us
    ppermute x2, waiting for transfers between devices, ring_near(): lax.ppermute(rows, PLANE, plane_perm(-1, x_core))  12 us
    ppermute x6, starting transfers between devices, swap(): return lax.ppermute(rows, 'core', [(0, 1), (1, 0)])  11.1 us
    ppermute x2, waiting for transfers between devices, ring_far(): lax.ppermute(right[:half], PLANE, plane_perm(1, x_core))  6.88 us
    unnamed x21, local copies, waits for them, and re-layouts  6.5 us
  transfers between devices with their start and end apart: 16, of which 7 were waited for; matrix products, arithmetic and copies ran while one was open for 5% of the time, Pallas kernels for 0%

commit v1 on v0

--- a/solution.py
+++ b/solution.py
@@ -13,6 +13,7 @@
 HALF = 512
 COLS = 1024
 MASKED = -1e30
+START = -1e29
 SLACK = 60.0
 OFFS = (0, -1, 1, 2)
 PLANE = ("xh", "y", "xl", "core")
@@ -60,18 +61,19 @@
 
 
 ALL8 = [(o, j) for o in range(4) for j in range(2)]
+A4, B4 = ALL8[:4], ALL8[4:]
 PARTS = (
-    (0, 0, 0, ALL8, 0),
-    (1, 0, 1, ALL8, 2), (2, 0, 2, ALL8, 4),
-    (1, 1, 1, ALL8, 6), (2, 1, 2, ALL8, 6),
-    (0, 1, 0, ALL8, 10), (3, 1, 3, ALL8[:4], 10), (4, 1, 3, ALL8[4:], 10),
-    (3, 0, 3, ALL8[:4], 14), (4, 0, 3, ALL8[4:], 14),
+    (0, 0, 0, A4, 0), (1, 0, 0, B4, 0),
+    (2, 0, 1, A4, 2), (4, 0, 1, B4, 2), (3, 0, 2, A4, 4), (5, 0, 2, B4, 4),
+    (2, 1, 1, A4, 6), (4, 1, 1, B4, 6), (3, 1, 2, A4, 6), (5, 1, 2, B4, 6),
+    (0, 1, 0, A4, 10), (1, 1, 0, B4, 10), (6, 1, 3, A4, 10), (7, 1, 3, B4, 10),
+    (6, 0, 3, A4, 14), (7, 0, 3, B4, 14),
 )
 
 
 def attend(seg_ref, idx_ref, q_ref, self_ref, *rest):
-    own_refs, swp_refs = rest[:5], rest[5:10]
-    o_ref, buf, qs, hbs, far, flag, sems, acc, mx, over, lim = rest[10:]
+    own_refs, swp_refs = rest[:8], rest[8:16]
+    o_ref, buf, qs, hbs, far, flag, sems, acc, mx, over, lim = rest[16:]
     z, xh, xl, y, core = [idx_ref[k] for k in range(5)]
     flip = jnp.where(z < 4, 0, 15)
     x = xh * 2 + xl
@@ -124,6 +126,7 @@
             lim[g, :, at] = jnp.maximum(qt * TILE + xh * 64 + (col & 63), limit)
         far[g] = reach
     acc[...] = jnp.zeros_like(acc)
+    over[...] = jnp.full_like(over, MASKED)
 
     def load(slot, count):
         rows = buf[pl.ds(slot, count)].reshape(count * 256, 256)
@@ -142,72 +145,85 @@
         return a.reshape(a.shape[0] // 8, 8, COLS)
 
     def quick(g, kk, vt, mask):
-        ref = mx[g]
         s = scores(g, kk, mask)
-        top = jnp.max(by_sublane(s), axis=0)
-        p = jnp.exp2(s - ref)
-        pv = jnp.dot(vt, p.astype(jnp.bfloat16), preferred_element_type=jnp.float32)
-        top = jnp.max(top, axis=0, keepdims=True) - ref
-        over[...] = top
-        good = top <= SLACK
-        acc[g] = acc[g] + jnp.where(good, pv, 0.0)
-        flag[0] = (jnp.max(top) > SLACK).astype(jnp.int32)
+        over[g] = jnp.maximum(over[g], jnp.max(by_sublane(s), axis=0))
+        p = jnp.exp2(s - mx[g])
+        acc[g] = acc[g] + jnp.dot(vt, p.astype(jnp.bfloat16), preferred_element_type=jnp.float32)
 
     def slow(g, kk, vt, mask):
-        todo = over[...] > SLACK
         s = scores(g, kk, mask)
         old = mx[g]
-        new = jnp.where(todo, jnp.maximum(old, jnp.max(s, axis=0, keepdims=True)), old)
-        alpha = jnp.exp2(old - new)
-        p = jnp.where(todo, jnp.exp2(s - new), 0.0)
+        new = jnp.maximum(old, jnp.max(s, axis=0, keepdims=True))
+        p = jnp.exp2(s - new)
         pv = jnp.dot(vt, p.astype(jnp.bfloat16), preferred_element_type=jnp.float32)
-        acc[g] = acc[g] * alpha + pv
+        acc[g] = acc[g] * jnp.exp2(old - new) + pv
         mx[g] = new
 
-    def both(g, slot, count, mask):
-        quick(g, *load(slot, count), mask)
-
-        @pl.when(flag[0] == 1)
+    def masked(g, unit, apply):
+        hb = hbs[unit]
+
+        @pl.when(hb <= far[g])
         def _():
-            slow(g, *load(slot, count), mask)
+            key = lax.broadcasted_iota(jnp.int32, (HALF, 128), 0)
+            kpos = hb * HALF + ((key & 255) >> 6) * TILE + (key >> 8) * 64 + (key & 63)
+            kpos = jnp.concatenate([kpos] * (COLS // 128), axis=1)
+            apply(g, *load(unit * 2, 2), kpos <= lim[g])
 
     def one_pair(p, c):
         for i in range(4):
             pltpu.make_async_copy(
                 own_refs[0].at[pl.ds(0, 256)], buf.at[p * 4 + i], sems.at[p * 4 + i]
             ).wait()
-        hb0, hb1 = hbs[p * 2], hbs[p * 2 + 1]
-
-        def one_group(g, c):
-            hbq = jnp.where(g == 0, n * 2, (15 - n) * 2 + 1)
-            dense = (hb0 < hbq) & (hb1 < hbq)
-
-            @pl.when(dense)
-            def _():
-                both(g, p * 4, 4, None)
-
-            @pl.when(jnp.logical_not(dense))
-            def _():
-                def masked(u, c):
-                    hb = hbs[p * 2 + u]
-
-                    @pl.when(hb <= far[g])
-                    def _():
-                        key = lax.broadcasted_iota(jnp.int32, (HALF, 128), 0)
-                        kpos = hb * HALF + ((key & 255) >> 6) * TILE + (key >> 8) * 64 + (key & 63)
-                        kpos = jnp.concatenate([kpos] * (COLS // 128), axis=1)
-                        both(g, p * 4 + u * 2, 2, kpos <= lim[g])
-
-                    return c
-
-                lax.fori_loop(0, 2, masked, 0)
-
+        hb = jnp.maximum(hbs[p * 2], hbs[p * 2 + 1])
+        first, second = hb < n * 2, hb < (15 - n) * 2 + 1
+
+        @pl.when(first & second)
+        def _():
+            kk, vt = load(p * 4, 4)
+            quick(0, kk, vt, None)
+            quick(1, kk, vt, None)
+
+        @pl.when(jnp.logical_not(first & second))
+        def _():
+            def one_group(g, c):
+                dense = jnp.where(g == 0, first, second)
+
+                @pl.when(dense)
+                def _():
+                    quick(g, *load(p * 4, 4), None)
+
+                @pl.when(jnp.logical_not(dense))
+                def _():
+                    def one_unit(u, c):
+                        masked(g, p * 2 + u, quick)
+                        return c
+
+                    lax.fori_loop(0, 2, one_unit, 0)
+
+                return c
+
+            lax.fori_loop(0, 2, one_group, 0)
+
+        return c
+
+    lax.fori_loop(0, 16, one_pair, 0)
+
+    excess = jnp.maximum(
+        jnp.max(over[0], axis=0, keepdims=True) - mx[0],
+        jnp.max(over[1], axis=0, keepdims=True) - mx[1],
+    )
+    flag[0] = (jnp.max(excess) > SLACK).astype(jnp.int32)
+
+    @pl.when(flag[0] == 1)
+    def _():
+        acc[...] = jnp.zeros_like(acc)
+        mx[...] = jnp.full_like(mx, START)
+
+        def again(i, c):
+            masked(i & 1, i >> 1, slow)
             return c
 
-        lax.fori_loop(0, 2, one_group, 0)
-        return c
-
-    lax.fori_loop(0, 16, one_pair, 0)
+        lax.fori_loop(0, 64, again, 0)
 
     for t in range(8):
         at = slice(t % 4 * 256, (t % 4 + 1) * 256)
@@ -233,19 +249,21 @@
     q = exchange(q)
     r1, l1 = ring_near(start, 0)
     f1 = ring_far(r1, l1, 0)
-    row = jnp.concatenate([start, r1, l1, *f1], axis=0)
-    r2, l2 = ring_near(row, 1)
-    row_s = swap(row)
-    f2 = ring_far(r2, l2, 1)
-    own = (row, r2, l2, *f2)
-    swp = (row_s, *[swap(o) for o in own[1:]])
+    row_a = jnp.concatenate([start, r1], axis=0)
+    row_b = jnp.concatenate([l1, *f1], axis=0)
+    ra, la = ring_near(row_a, 1)
+    rb, lb = ring_near(row_b, 1)
+    fa = lax.ppermute(ra, PLANE, plane_perm(1, 1))
+    fb = lax.ppermute(lb, PLANE, plane_perm(-1, 1))
+    own = (row_a, row_b, ra, la, rb, lb, fa, fb)
+    swp = tuple(swap(o) for o in own)
 
     smem = pl.BlockSpec(memory_space=pltpu.SMEM)
     vmem = pl.BlockSpec(memory_space=pltpu.VMEM)
     out = pl.pallas_call(
         attend,
         out_shape=jax.ShapeDtypeStruct((8, 64, 512), jnp.bfloat16),
-        in_specs=[smem, smem, vmem, vmem] + [pl.BlockSpec(memory_space=pl.ANY)] * 10,
+        in_specs=[smem, smem, vmem, vmem] + [pl.BlockSpec(memory_space=pltpu.HBM)] * 16,
         out_specs=vmem,
         scratch_shapes=[
             pltpu.VMEM((64, 256, 256), jnp.bfloat16),
@@ -256,7 +274,7 @@
             pltpu.SemaphoreType.DMA((64,)),
             pltpu.VMEM((2, 144, COLS), jnp.float32),
             pltpu.VMEM((2, 1, COLS), jnp.float32),
-            pltpu.VMEM((1, COLS), jnp.float32),
+            pltpu.VMEM((2, 8, COLS), jnp.float32),
             pltpu.VMEM((2, 1, COLS), jnp.int32),
         ],
         name="attend",

time: 143 us -> 160 us (1.12)
  the two profiles are of different devices: /device:TPU:1 before, /device:TPU:62 now
where the time goes in v1:
time: 160 us
  Pallas kernels  59 us (37%)
  waiting for transfers between devices  47.5 us (30%)
  starting transfers between devices  28 us (18%)
  blocking collectives  17.6 us (11%)
  local copies, waits for them, and re-layouts  6.89 us (4%)
    pallas_call x1, Pallas kernels, local(): pl.pallas_call(attend, out_shape=jax.ShapeDtypeStruct((8, 64, 512), jnp.b...  59 us
    all_to_all x2, waiting for transfers between devices, exchange(): lax.all_to_all(rows, ROUND, split_axis=0, concat_axis=0, axis_index_group...  24.1 us
    all_to_all x1, blocking collectives, exchange(): lax.all_to_all(rows, ROUND, split_axis=0, concat_axis=0, axis_index_group...  17.6 us
    all_to_all x2, starting transfers between devices, exchange(): lax.all_to_all(rows, ROUND, split_axis=0, concat_axis=0, axis_index_group...  12.1 us
    ppermute x3, starting transfers between devices, ring_near(): lax.ppermute(rows, PLANE, plane_perm(1, x_core))  7.64 us
    ppermute x3, waiting for transfers between devices, ring_near(): lax.ppermute(rows, PLANE, plane_perm(-1, x_core))  6.63 us
    ppermute x1, waiting for transfers between devices, ring_far(): lax.ppermute(left[half:], PLANE, plane_perm(-1, x_core))  6.62 us
    ppermute x1, waiting for transfers between devices, local(): fb = lax.ppermute(lb, PLANE, plane_perm(-1, 1))  5.56 us
  transfers between devices with their start and end apart: 21, of which 7 were waited for; matrix products, arithmetic and copies ran while one was open for 1% of the time, Pallas kernels for 0%

profile of v1, /device:TPU:62, one launch (start us, length us, event | category | flops | bytes accessed | tf_op | source)
XLA Modules:
  0.0 160.1 jit_solution(9100354655148852418)
XLA Ops:
  0.0 0.9 copy.10
  1.0 0.9 copy-done.11
  1.9 0.7 maximum_bitcast_fusion
  2.6 8.1 %all-to-all-start = ((bf16[8,64,256]{2,1,0:T(8,128)(2,1)}), bf16[8,64,256]{2,1,0:T(8,128)(2,1)S(1)}, u32[]{:S(2)}, u32[]{:S(2)}) async-start(bf16[8,64,256]{2,1,0:T(8,128)(2,1)} %maximum_bitcast_fusion), calls=%async_computation | async-start | bytes 524288 | tf_op jit(solution)/shard_map/all_to_all | solution.py:25
  10.7 12.6 %all-to-all-done.self_ref = bf16[8,64,256]{2,1,0:T(8,128)(2,1)S(1)} async-done(((bf16[8,64,256]{2,1,0:T(8,128)(2,1)}), bf16[8,64,256]{2,1,0:T(8,128)(2,1)S(1)}, u32[]{:S(2)}, u32[]{:S(2)}) %all-to-all-start) | async-done | bytes 262176 | tf_op jit(solution)/shard_map/all_to_all | solution.py:25
  24.0 1.5 collective-permute-start
  25.6 0.9 copy.13
  26.6 1.2 collective-permute-start.1
  27.8 0.9 collective-permute-start.2
  28.7 4.3 %collective-permute-done.1 = bf16[512,256]{1,0:T(8,128)(2,1)S(1)} collective-permute-done((bf16[512,256]{1,0:T(8,128)(2,1)S(1)}, bf16[512,256]{1,0:T(8,128)(2,1)S(1)}, u32[]{:S(2)}, u32[]{:S(2)}) %collective-permute-start.1) | collective-permute-done | bytes 262176 | tf_op jit(solution)/shard_map/ppermute | solution.py:46
  33.1 2.4 %collective-permute-start.3 = (bf16[256,256]{1,0:T(8,128)(2,1)S(1)}, bf16[256,256]{1,0:T(8,128)(2,1)S(1)}, u32[]{:S(2)}, u32[]{:S(2)}) collective-permute-start(bf16[256,256]{1,0:T(8,128)(2,1)S(1)} %slice.8), channel_id=1, source_target_pairs={{0,2},{1,5},{2,16},{3,7},{4,6},{5,9},{6,20},{7,11},{8,10},{9,13},{... | collective-permute-start | bytes 393224 | tf_op jit(solution)/shard_map/ppermute | solution.py:54
  35.5 1.0 collective-permute-start.11
  36.6 3.2 %collective-permute-start.5 = (bf16[1024,256]{1,0:T(8,128)(2,1)S(1)}, bf16[1024,256]{1,0:T(8,128)(2,1)S(1)}, u32[]{:S(2)}, u32[]{:S(2)}) collective-permute-start(bf16[1024,256]{1,0:T(8,128)(2,1)S(1)} %constant_dynamic-update-slice_fusion.rest_0_), channel_id=1, source_target_pairs={{0,4},{1,3},{2,6},{3,17},{4,8},{5,7},{6,10},{7,21},{8,12},{9,11},{... | collective-permute-start | bytes 1572872 | tf_op jit(solution)/shard_map/ppermute | solution.py:46
  39.8 1.0 collective-permute-start.4
  40.9 6.6 %collective-permute-done.4 = bf16[256,256]{1,0:T(8,128)(2,1)S(1)} collective-permute-done((bf16[256,256]{1,0:T(8,128)(2,1)S(1)}, bf16[256,256]{1,0:T(8,128)(2,1)S(1)}, u32[]{:S(2)}, u32[]{:S(2)}) %collective-permute-start.4) | collective-permute-done | bytes 131104 | tf_op jit(solution)/shard_map/ppermute | solution.py:55
  47.7 3.2 %collective-permute-start.7 = (bf16[1024,256]{1,0:T(8,128)(2,1)S(1)}, bf16[1024,256]{1,0:T(8,128)(2,1)}, u32[]{:S(2)}, u32[]{:S(2)}) collective-permute-start(bf16[1024,256]{1,0:T(8,128)(2,1)S(1)} %constant_dynamic-update-slice_fusion.2.rest_1_), channel_id=1, source_target_pairs={{0,4},{1,3},{2,6},{3,17},{4,8},{5,7},{6,10},{7,21},{8,12},{9,11},{... | collective-permute-start | bytes 1572872 | tf_op jit(solution)/shard_map/ppermute | solution.py:46
  51.5 6.6 %collective-permute-done.8.rest_5_ = bf16[1024,256]{1,0:T(8,128)(2,1)} collective-permute-done((bf16[1024,256]{1,0:T(8,128)(2,1)S(1)}, bf16[1024,256]{1,0:T(8,128)(2,1)}, u32[]{:S(2)}, u32[]{:S(2)}) %collective-permute-start.8) | collective-permute-done | bytes 524320 | tf_op jit(solution)/shard_map/ppermute | solution.py:47
  58.1 4.0 %all-to-all-start.1 = ((bf16[8,64,512]{2,1,0:T(8,128)(2,1)}), bf16[8,64,512]{2,1,0:T(8,128)(2,1)S(1)}, u32[]{:S(2)}, u32[]{:S(2)}) async-start(bf16[8,64,512]{2,1,0:T(8,128)(2,1)} %bitcast.20), calls=%async_computation.1 | async-start | bytes 1048576 | tf_op jit(solution)/shard_map/all_to_all | solution.py:25
  63.2 5.6 %collective-permute-done.10.rest_7_ = bf16[1024,256]{1,0:T(8,128)(2,1)} collective-permute-done((bf16[1024,256]{1,0:T(8,128)(2,1)}, bf16[1024,256]{1,0:T(8,128)(2,1)}, u32[]{:S(2)}, u32[]{:S(2)}) %collective-permute-start.10) | collective-permute-done | bytes 524320 | tf_op jit(solution)/shard_map/ppermute | solution.py:257
  69.5 11.5 %all-to-all-done.1.q_ref = bf16[8,64,512]{2,1,0:T(8,128)(2,1)S(1)} async-done(((bf16[8,64,512]{2,1,0:T(8,128)(2,1)}), bf16[8,64,512]{2,1,0:T(8,128)(2,1)S(1)}, u32[]{:S(2)}, u32[]{:S(2)}) %all-to-all-start.1) | async-done | bytes 524320 | tf_op jit(solution)/shard_map/all_to_all | solution.py:25
  81.0 0.7 copy-done.1
  82.1 59.0 %attend.1 = bf16[8,64,512]{2,1,0:T(8,128)(2,1)} custom-call(s32[128]{0:T(128)} %seg_ref.1, s32[5]{0:T(128)} %stack.23.idx_ref, bf16[8,64,512]{2,1,0:T(8,128)(2,1)} %copy-done.1, bf16[8,64,256]{2,1,0:T(8,128)(2,1)} %copy-done, bf16[1024,256]{1,0:T(8,128)(2,1)} %copy-done.2, bf16[1024,256]{1,0:T(8,128)(2,1)} %copy-done.3, bf16[1024,256]{1,0:T(8,128)(2,1)} %copy-done.6, ...), custom_call_target="tpu_custom_call" | custom-call | tf_op jit(solution)/shard_map/attend/pallas_call | solution.py:263
  141.2 17.6 %all_to_all.15 = bf16[8,64,512]{2,1,0:T(8,128)(2,1)S(1)} all-to-all(bf16[8,64,512]{2,1,0:T(8,128)(2,1)} %attend.1), channel_id=1, replica_groups={{0,32,64,96,143,175,207,239},{1,33,65,97,142,174,206,238},{2,34,66,98,1..., dimensions={0} | all-to-all | bytes 1048576 | tf_op jit(solution)/shard_map/all_to_all | solution.py:25
  159.0 1.0 reshape.7
  (63 shorter events, 4.3 us)
Async XLA Ops:
  2.6 22.8 %copy-start.10 = (bf16[1,64,4096]{2,1,0:T(8,128)(2,1)S(1)}, bf16[1,64,4096]{2,1,0:T(8,128)(2,1)}, u32[]{:S(2)}) copy-start(bf16[1,64,4096]{2,1,0:T(8,128)(2,1)} %param.4) | copy-start | bytes 1572868
  2.6 20.6 %all-to-all-start = ((bf16[8,64,256]{2,1,0:T(8,128)(2,1)}), bf16[8,64,256]{2,1,0:T(8,128)(2,1)S(1)}, u32[]{:S(2)}, u32[]{:S(2)}) async-start(bf16[8,64,256]{2,1,0:T(8,128)(2,1)} %maximum_bitcast_fusion), calls=%async_computation | async-start | bytes 524288 | tf_op jit(solution)/shard_map/all_to_all | solution.py:25
  24.0 2.6 %collective-permute-start = (bf16[256,256]{1,0:T(8,128)(2,1)S(1)}, bf16[256,256]{1,0:T(8,128)(2,1)S(1)}, u32[]{:S(2)}, u32[]{:S(2)}) collective-permute-start(bf16[256,256]{1,0:T(8,128)(2,1)S(1)} %get-tuple-element.10), channel_id=1, source_target_pairs={{0,1},{1,0},{2,3},{3,2},{4,5},{5,4},{6,7},{7,6},{8,9},{9,8},{10,11... | collective-permute-start | bytes 393224 | tf_op jit(solution)/shard_map/ppermute | solution.py:60
  26.6 6.4 %collective-permute-start.1 = (bf16[512,256]{1,0:T(8,128)(2,1)S(1)}, bf16[512,256]{1,0:T(8,128)(2,1)S(1)}, u32[]{:S(2)}, u32[]{:S(2)}) collective-permute-start(bf16[512,256]{1,0:T(8,128)(2,1)S(1)} %pad_maximum_fusion), channel_id=1, source_target_pairs={{0,2},{1,5},{2,16},{3,7},{4,6},{5,9},{6,20},{7,11},{8,10},{9,13},{... | collective-permute-start | bytes 786440 | tf_op jit(solution)/shard_map/ppermute | solution.py:46
  27.8 12.0 %collective-permute-start.2 = (bf16[512,256]{1,0:T(8,128)(2,1)S(1)}, bf16[512,256]{1,0:T(8,128)(2,1)S(1)}, u32[]{:S(2)}, u32[]{:S(2)}) collective-permute-start(bf16[512,256]{1,0:T(8,128)(2,1)S(1)} %pad_maximum_fusion), channel_id=1, source_target_pairs={{0,18},{1,13},{2,0},{3,15},{4,22},{5,1},{6,4},{7,3},{8,26},{9,5},{... | collective-permute-start | bytes 786440 | tf_op jit(solution)/shard_map/ppermute | solution.py:47
  33.1 7.8 %collective-permute-start.3 = (bf16[256,256]{1,0:T(8,128)(2,1)S(1)}, bf16[256,256]{1,0:T(8,128)(2,1)S(1)}, u32[]{:S(2)}, u32[]{:S(2)}) collective-permute-start(bf16[256,256]{1,0:T(8,128)(2,1)S(1)} %slice.8), channel_id=1, source_target_pairs={{0,2},{1,5},{2,16},{3,7},{4,6},{5,9},{6,20},{7,11},{8,10},{9,13},{... | collective-permute-start | bytes 393224 | tf_op jit(solution)/shard_map/ppermute | solution.py:54
  35.5 12.2 %collective-permute-start.11 = (bf16[1024,256]{1,0:T(8,128)(2,1)S(1)}, bf16[1024,256]{1,0:T(8,128)(2,1)S(1)}, u32[]{:S(2)}, u32[]{:S(2)}) collective-permute-start(bf16[1024,256]{1,0:T(8,128)(2,1)S(1)} %constant_dynamic-update-slice_fusion.rest_0_), channel_id=1, source_target_pairs={{0,1},{1,0},{2,3},{3,2},{4,5},{5,4},{6,7},{7,6},{8,9},{9,8},{10,11... | collective-permute-start | bytes 1572872 | tf_op jit(solution)/shard_map/ppermute | solution.py:60
  36.6 14.3 %collective-permute-start.6 = (bf16[1024,256]{1,0:T(8,128)(2,1)S(1)}, bf16[1024,256]{1,0:T(8,128)(2,1)S(1)}, u32[]{:S(2)}, u32[]{:S(2)}) collective-permute-start(bf16[1024,256]{1,0:T(8,128)(2,1)S(1)} %constant_dynamic-update-slice_fusion.rest_0_), channel_id=1, source_target_pairs={{0,12},{1,19},{2,14},{3,1},{4,0},{5,23},{6,2},{7,5},{8,4},{9,27},{... | collective-permute-start | bytes 1572872 | tf_op jit(solution)/shard_map/ppermute | solution.py:47
  36.6 14.3 %collective-permute-start.5 = (bf16[1024,256]{1,0:T(8,128)(2,1)S(1)}, bf16[1024,256]{1,0:T(8,128)(2,1)S(1)}, u32[]{:S(2)}, u32[]{:S(2)}) collective-permute-start(bf16[1024,256]{1,0:T(8,128)(2,1)S(1)} %constant_dynamic-update-slice_fusion.rest_0_), channel_id=1, source_target_pairs={{0,4},{1,3},{2,6},{3,17},{4,8},{5,7},{6,10},{7,21},{8,12},{9,11},{... | collective-permute-start | bytes 1572872 | tf_op jit(solution)/shard_map/ppermute | solution.py:46
  39.8 7.7 %collective-permute-start.4 = (bf16[256,256]{1,0:T(8,128)(2,1)S(1)}, bf16[256,256]{1,0:T(8,128)(2,1)S(1)}, u32[]{:S(2)}, u32[]{:S(2)}) collective-permute-start(bf16[256,256]{1,0:T(8,128)(2,1)S(1)} %slice.9), channel_id=1, source_target_pairs={{0,18},{1,13},{2,0},{3,15},{4,22},{5,1},{6,4},{7,3},{8,26},{9,5},{... | collective-permute-start | bytes 393224 | tf_op jit(solution)/shard_map/ppermute | solution.py:55
  47.5 10.6 %collective-permute-start.8 = (bf16[1024,256]{1,0:T(8,128)(2,1)S(1)}, bf16[1024,256]{1,0:T(8,128)(2,1)}, u32[]{:S(2)}, u32[]{:S(2)}) collective-permute-start(bf16[1024,256]{1,0:T(8,128)(2,1)S(1)} %constant_dynamic-update-slice_fusion.2.rest_1_), channel_id=1, source_target_pairs={{0,12},{1,19},{2,14},{3,1},{4,0},{5,23},{6,2},{7,5},{8,4},{9,27},{... | collective-permute-start | bytes 1572872 | tf_op jit(solution)/shard_map/ppermute | solution.py:47
  47.6 14.5 %collective-permute-start.12 = (bf16[1024,256]{1,0:T(8,128)(2,1)S(1)}, bf16[1024,256]{1,0:T(8,128)(2,1)}, u32[]{:S(2)}, u32[]{:S(2)}) collective-permute-start(bf16[1024,256]{1,0:T(8,128)(2,1)S(1)} %constant_dynamic-update-slice_fusion.2.rest_1_), channel_id=1, source_target_pairs={{0,1},{1,0},{2,3},{3,2},{4,5},{5,4},{6,7},{7,6},{8,9},{9,8},{10,11... | collective-permute-start | bytes 1572872 | tf_op jit(solution)/shard_map/ppermute | solution.py:60
  47.7 14.4 %collective-permute-start.7 = (bf16[1024,256]{1,0:T(8,128)(2,1)S(1)}, bf16[1024,256]{1,0:T(8,128)(2,1)}, u32[]{:S(2)}, u32[]{:S(2)}) collective-permute-start(bf16[1024,256]{1,0:T(8,128)(2,1)S(1)} %constant_dynamic-update-slice_fusion.2.rest_1_), channel_id=1, source_target_pairs={{0,4},{1,3},{2,6},{3,17},{4,8},{5,7},{6,10},{7,21},{8,12},{9,11},{... | collective-permute-start | bytes 1572872 | tf_op jit(solution)/shard_map/ppermute | solution.py:46
  50.9 30.1 %copy-start.5 = (bf16[1024,256]{1,0:T(8,128)(2,1)}, bf16[1024,256]{1,0:T(8,128)(2,1)S(1)}, u32[]{:S(2)}) copy-start(bf16[1024,256]{1,0:T(8,128)(2,1)S(1)} %collective-permute-done.6.rest_3_) | copy-start | bytes 1572868
  50.9 11.7 %collective-permute-start.14 = (bf16[1024,256]{1,0:T(8,128)(2,1)S(1)}, bf16[1024,256]{1,0:T(8,128)(2,1)}, u32[]{:S(2)}, u32[]{:S(2)}) collective-permute-start(bf16[1024,256]{1,0:T(8,128)(2,1)S(1)} %collective-permute-done.6.rest_3_), channel_id=1, source_target_pairs={{0,1},{1,0},{2,3},{3,2},{4,5},{5,4},{6,7},{7,6},{8,9},{9,8},{10,11... | collective-permute-start | bytes 1572872 | tf_op jit(solution)/shard_map/ppermute | solution.py:60
  50.9 30.1 %copy-start.6 = (bf16[1024,256]{1,0:T(8,128)(2,1)}, bf16[1024,256]{1,0:T(8,128)(2,1)S(1)}, u32[]{:S(2)}) copy-start(bf16[1024,256]{1,0:T(8,128)(2,1)S(1)} %collective-permute-done.5.rest_2_) | copy-start | bytes 1572868
  51.0 12.3 %collective-permute-start.9 = (bf16[1024,256]{1,0:T(8,128)(2,1)S(1)}, bf16[1024,256]{1,0:T(8,128)(2,1)S(1)}, u32[]{:S(2)}, u32[]{:S(2)}) collective-permute-start(bf16[1024,256]{1,0:T(8,128)(2,1)S(1)} %collective-permute-done.5.rest_2_), channel_id=1, source_target_pairs={{0,4},{1,3},{2,6},{3,17},{4,8},{5,7},{6,10},{7,21},{8,12},{9,11},{... | collective-permute-start | bytes 1572872 | tf_op jit(solution)/shard_map/ppermute | solution.py:256
  58.1 10.7 %collective-permute-start.10 = (bf16[1024,256]{1,0:T(8,128)(2,1)}, bf16[1024,256]{1,0:T(8,128)(2,1)}, u32[]{:S(2)}, u32[]{:S(2)}) collective-permute-start(bf16[1024,256]{1,0:T(8,128)(2,1)} %collective-permute-done.8.rest_5_), channel_id=1, source_target_pairs={{0,12},{1,19},{2,14},{3,1},{4,0},{5,23},{6,2},{7,5},{8,4},{9,27},{... | collective-permute-start | bytes 1572872 | tf_op jit(solution)/shard_map/ppermute | solution.py:257
  58.1 22.9 %all-to-all-start.1 = ((bf16[8,64,512]{2,1,0:T(8,128)(2,1)}), bf16[8,64,512]{2,1,0:T(8,128)(2,1)S(1)}, u32[]{:S(2)}, u32[]{:S(2)}) async-start(bf16[8,64,512]{2,1,0:T(8,128)(2,1)} %bitcast.20), calls=%async_computation.1 | async-start | bytes 1048576 | tf_op jit(solution)/shard_map/all_to_all | solution.py:25
  62.1 18.8 %collective-permute-start.13 = (bf16[1024,256]{1,0:T(8,128)(2,1)S(1)}, bf16[1024,256]{1,0:T(8,128)(2,1)S(1)}, u32[]{:S(2)}, u32[]{:S(2)}) collective-permute-start(bf16[1024,256]{1,0:T(8,128)(2,1)S(1)} %collective-permute-done.5.rest_2_), channel_id=1, source_target_pairs={{0,1},{1,0},{2,3},{3,2},{4,5},{5,4},{6,7},{7,6},{8,9},{9,8},{10,11... | collective-permute-start | bytes 1572872 | tf_op jit(solution)/shard_map/ppermute | solution.py:60
  62.1 18.8 %collective-permute-start.16 = (bf16[1024,256]{1,0:T(8,128)(2,1)}, bf16[1024,256]{1,0:T(8,128)(2,1)S(1)}, u32[]{:S(2)}, u32[]{:S(2)}) collective-permute-start(bf16[1024,256]{1,0:T(8,128)(2,1)} %collective-permute-done.8.rest_5_), channel_id=1, source_target_pairs={{0,1},{1,0},{2,3},{3,2},{4,5},{5,4},{6,7},{7,6},{8,9},{9,8},{10,11... | collective-permute-start | bytes 1572872 | tf_op jit(solution)/shard_map/ppermute | solution.py:60
  62.6 18.3 %collective-permute-start.15 = (bf16[1024,256]{1,0:T(8,128)(2,1)}, bf16[1024,256]{1,0:T(8,128)(2,1)}, u32[]{:S(2)}, u32[]{:S(2)}) collective-permute-start(bf16[1024,256]{1,0:T(8,128)(2,1)} %collective-permute-done.7.rest_4_), channel_id=1, source_target_pairs={{0,1},{1,0},{2,3},{3,2},{4,5},{5,4},{6,7},{7,6},{8,9},{9,8},{10,11... | collective-permute-start | bytes 1572872 | tf_op jit(solution)/shard_map/ppermute | solution.py:60
  63.2 17.8 %collective-permute-start.17 = (bf16[1024,256]{1,0:T(8,128)(2,1)S(1)}, bf16[1024,256]{1,0:T(8,128)(2,1)}, u32[]{:S(2)}, u32[]{:S(2)}) collective-permute-start(bf16[1024,256]{1,0:T(8,128)(2,1)S(1)} %collective-permute-done.9.rest_6_), channel_id=1, source_target_pairs={{0,1},{1,0},{2,3},{3,2},{4,5},{5,4},{6,7},{7,6},{8,9},{9,8},{10,11... | collective-permute-start | bytes 1572872 | tf_op jit(solution)/shard_map/ppermute | solution.py:60
  68.8 12.2 %collective-permute-start.18 = (bf16[1024,256]{1,0:T(8,128)(2,1)}, bf16[1024,256]{1,0:T(8,128)(2,1)}, u32[]{:S(2)}, u32[]{:S(2)}) collective-permute-start(bf16[1024,256]{1,0:T(8,128)(2,1)} %collective-permute-done.10.rest_7_), channel_id=1, source_target_pairs={{0,1},{1,0},{2,3},{3,2},{4,5},{5,4},{6,7},{7,6},{8,9},{9,8},{10,11... | collective-permute-start | bytes 1572872 | tf_op jit(solution)/shard_map/ppermute | solution.py:60
  (9 other events, 48.7 us)
